TPU v7x, 256 devices: a whole 4x4x8 slice. The times are simulated.
256 devices in a mesh: job: 4 (over y), zero: 16 (over z, core), cols: 4 (over x).
Axes of the slice: x: 4, y: 4, z: 8, core: 2. Of those that a mesh axis runs over, the one named last changes fastest.
Arguments:
- weight_query: bfloat16 [12288, 3072], P(('job', 'zero'), 'cols'), parts along dimension 0, may hold values from -0.109375 to 0.109375
- low_query: bfloat16 [12288, 32], P(('job', 'zero')), parts along dimension 0, may hold values from -0.109375 to 0.109375
- high_query: bfloat16 [128, 3072], P('job', 'cols'), parts along dimension 0, may hold values from -1 to 1
- weight_key: bfloat16 [12288, 1024], P(('job', 'zero'), 'cols'), parts along dimension 0, may hold values from -0.109375 to 0.109375
- low_key: bfloat16 [12288, 32], P(('job', 'zero')), parts along dimension 0, may hold values from -0.109375 to 0.109375
- high_key: bfloat16 [128, 1024], P('job', 'cols'), parts along dimension 0, may hold values from -1 to 1
- weight_value: bfloat16 [12288, 1024], P(('job', 'zero'), 'cols'), parts along dimension 0, may hold values from -0.109375 to 0.109375
- low_value: bfloat16 [12288, 32], P(('job', 'zero')), parts along dimension 0, may hold values from -0.109375 to 0.109375
- high_value: bfloat16 [128, 1024], P('job', 'cols'), parts along dimension 0, may hold values from -1 to 1
- weight_mixed: bfloat16 [12288, 3072], P(('job', 'cols'), 'zero'), parts along dimension 0, may hold values from -0.109375 to 0.109375
- low_mixed: bfloat16 [12288, 32], P(('job', 'cols')), parts along dimension 0, may hold values from -0.109375 to 0.109375
- high_mixed: bfloat16 [128, 3072], P('job', 'zero'), parts along dimension 0, may hold values from -1 to 1
- norm_train: float32 [12288], P(('job', 'zero', 'cols')), parts along dimension 0, may hold values from 0.25 to 1.75
- norm_step: float32 [12288], P(('job', 'zero', 'cols')), parts along dimension 0, may hold values from -0.3 to 0.3
Outputs:
- serving_query: bfloat16 [12288, 3072], P('job', 'cols'), parts along dimension 0
- serving_key: bfloat16 [12288, 1024], P('job', 'cols'), parts along dimension 0
- serving_value: bfloat16 [12288, 1024], P('job', 'cols'), parts along dimension 0
- serving_mixed: bfloat16 [12288, 3072], P(('job', 'cols')), parts along dimension 0
- serve_norm: bfloat16 [12288], P('job'), parts along dimension 0
There are 4 independent parts, one for each index of `job`. A program takes and returns all parts, laid end to end along the dimension named above; each array names one. Nothing has to cross between parts.
All inputs are finite; a program needn't handle non-finite values.
Results may differ from a plain program's by a relative error of at most 0.001.
Values may be sent and summed in bfloat16 or wider, within the bound.
A program may use at most 128 MiB of HBM per device.

v0:
```python
import jax
import jax.numpy as jnp
from jax import lax
from jax.sharding import PartitionSpec as P

mix_rate = 2.0


def gather_turned(arrays, axis, dims):
    turned = [jnp.moveaxis(a, dim, 0) for a, dim in zip(arrays, dims)]
    widths = [t[0].size for t in turned]
    both = jnp.concatenate([t.reshape(-1, w) for t, w in zip(turned, widths)], axis=1)
    whole = lax.all_gather(both, axis, axis=0, tiled=True)
    tiles = jnp.split(whole, [sum(widths[:k]) for k in range(1, len(widths))], axis=1)
    return tuple(
        (
            jnp.moveaxis(b.reshape(-1, *t.shape[1:]), 0, dim)
            for b, t, dim in zip(tiles, turned, dims)
        )
    )


def sent_to_all(array, axis):
    copies = jnp.broadcast_to(array, (lax.axis_size(axis), *array.shape))
    return lax.all_to_all(copies, axis, split_axis=0, concat_axis=0, tiled=True)


def joined_along(tiles, dim):
    tiles = jnp.moveaxis(tiles, 0, dim)
    dims = tiles.shape
    return tiles.reshape(*dims[:dim], dims[dim] * dims[dim + 1], *dims[dim + 2 :])


def collect(array, axis, dim):
    tiles = sent_to_all(array, axis)
    return joined_along(tiles, dim)


def on_device(
    weight_query,
    low_query,
    high_query,
    weight_key,
    low_key,
    high_key,
    weight_value,
    low_value,
    high_value,
    weight_mixed,
    low_mixed,
    high_mixed,
    norm_train,
    norm_step,
):
    whole_query = weight_query.astype(jnp.float32) + mix_rate * jnp.dot(
        low_query, high_query, preferred_element_type=jnp.float32
    )
    whole_key = weight_key.astype(jnp.float32) + mix_rate * jnp.dot(
        low_key, high_key, preferred_element_type=jnp.float32
    )
    whole_value = weight_value.astype(jnp.float32) + mix_rate * jnp.dot(
        low_value, high_value, preferred_element_type=jnp.float32
    )
    whole_mixed = weight_mixed.astype(jnp.float32) + mix_rate * jnp.dot(
        low_mixed, high_mixed, preferred_element_type=jnp.float32
    )
    narrow_query, narrow_key, narrow_value, narrow_mixed = (
        whole_query.astype(jnp.bfloat16),
        whole_key.astype(jnp.bfloat16),
        whole_value.astype(jnp.bfloat16),
        whole_mixed.astype(jnp.bfloat16),
    )
    serving_query, serving_key, serving_value, serving_mixed = gather_turned(
        (narrow_query, narrow_key, narrow_value, narrow_mixed), "zero", (0, 0, 0, 1)
    )
    serve_norm = collect((norm_train + norm_step).astype(jnp.bfloat16), ("zero", "cols"), 0)
    return (serving_query, serving_key, serving_value, serving_mixed, serve_norm)


def solution(mesh):
    placed = (
        P(("job", "zero"), "cols"),
        P(("job", "zero"), None),
        P("job", "cols"),
        P(("job", "zero"), "cols"),
        P(("job", "zero"), None),
        P("job", "cols"),
        P(("job", "zero"), "cols"),
        P(("job", "zero"), None),
        P("job", "cols"),
        P(("job", "cols"), "zero"),
        P(("job", "cols"), None),
        P("job", "zero"),
        P(("job", "zero", "cols")),
        P(("job", "zero", "cols")),
    )
    return jax.shard_map(
        on_device,
        mesh=mesh,
        in_specs=placed,
        out_specs=(
            P("job", "cols"),
            P("job", "cols"),
            P("job", "cols"),
            P(("job", "cols"), None),
            P("job"),
        ),
        check_vma=False,
    )
```

profile of v0, /device:TPU:1, one launch (start us, length us, event | category | flops | bytes accessed | tf_op | source)
XLA Modules:
  0.0 119.2 jit_solution(13461833786214713967)
XLA Ops:
  7.2 0.0 copy-start
  7.2 0.0 all-gather.2.cloned.1.call-start
  7.2 0.7 copy-done
  8.0 1.3 %fusion.4 = bf16[192,768]{1,0:T(8,128)(2,1)S(1)} fusion(bf16[768,32]{0,1:T(8,128)(2,1)S(1)} %copy-done, bf16[32,192]{1,0:T(8,128)(2,1)} %param.25, bf16[768,192]{0,1:T(8,128)(2,1)} %param.23), kind=kOutput, calls=%fused_computation.7 | convolution fusion | flops 10027008 | bytes 651264 | tf_op jit(solution)/shard_map/dot_general | solution.py:64
  9.2 1.1 fusion.8
  10.4 0.0 copy-start.1
  10.4 0.0 copy-start.2
  10.4 1.1 fusion.7
  11.6 1.3 %fusion.2 = bf16[192,768]{1,0:T(8,128)(2,1)S(1)} fusion(bf16[192,32]{0,1:T(8,128)(2,1)} %param.15, bf16[32,768]{1,0:T(8,128)(2,1)} %param.16, bf16[192,768]{1,0:T(8,128)(2,1)} %param.14), kind=kOutput, calls=%fused_computation.5 | convolution fusion | flops 10027008 | bytes 651264 | tf_op jit(solution)/shard_map/dot_general | solution.py:55
  12.8 1.0 pad_maximum_fusion
  13.8 0.0 all-gather.2.cloned.1.call-update
  13.8 0.0 copy-done.1
  13.8 0.0 copy-done.2
  13.9 22.0 %all_to_all.6 = bf16[64,1,48]{2,1,0:T(2,128)(2,1)S(1)} all-to-all(bf16[64,1,48]{2,1,0:T(2,128)(2,1)S(1)} %broadcast_in_dim.3), channel_id=1, replica_groups=mesh['job'=4,'zero'=16,'cols'=4] {'zero','cols'}, dimensions={0} | all-to-all | bytes 12288 | tf_op jit(solution)/shard_map/all_to_all | solution.py:25
  35.8 0.1 reduce
  35.9 0.7 reshape.18
  36.6 57.3 %all-gather.2.cloned.1.call-done = bf16[3072,2048]{1,0:T(8,128)(2,1)} async-done(((bf16[192,2048]{1,0:T(8,128)(2,1)}), bf16[3072,2048]{1,0:T(8,128)(2,1)}) %all-gather.2.cloned.1.call-update) | async-done | bytes 12582928 | tf_op jit(solution)/shard_map/all_gather | solution.py:13
  93.9 8.1 %slice_bitcast_fusion = (bf16[768,3072]{0,1:T(8,128)(2,1)}, bf16[3072,768]{1,0:T(8,128)(2,1)}) fusion(bf16[3072,2048]{1,0:T(8,128)(2,1)} %all-gather.2.cloned.1.call-done), kind=kLoop, calls=%fused_computation | loop fusion | bytes 18874368 | tf_op jit(solution)/shard_map/transpose | solution.py:17
  102.0 6.6 %copy.21 = bf16[768,3072]{1,0:T(8,128)(2,1)} copy(bf16[768,3072]{0,1:T(8,128)(2,1)} %get-tuple-element.20) | data formatting | bytes 9437184
  108.6 3.8 %fusion.9 = (bf16[3072,256]{1,0:T(8,128)(2,1)}, bf16[3072,256]{1,0:T(8,128)(2,1)}) fusion(bf16[3072,2048]{1,0:T(8,128)(2,1)} %all-gather.2.cloned.1.call-done), kind=kLoop, calls=%fused_computation.16 | loop fusion | bytes 6291456 | tf_op jit(solution)/shard_map/split | solution.py:14
  (2 shorter events, 0.0 us)
Async XLA Ops:
  7.2 0.8 copy-start
  7.2 86.7 %all-gather.2.cloned.1.call-start = ((), (), s32[]{:S(2)}) async-start(), calls=%async_computation.1 | async-start | bytes 13369344 | tf_op jit(solution)/shard_map/all_gather | solution.py:13
  10.4 3.4 %copy-start.1 = (f32[48]{0:T(128)S(1)}, f32[48]{0:T(128)}, u32[]{:S(2)}) copy-start(f32[48]{0:T(128)} %param.26) | copy-start | bytes 580
  10.4 3.4 %copy-start.2 = (f32[48]{0:T(128)S(1)}, f32[48]{0:T(128)}, u32[]{:S(2)}) copy-start(f32[48]{0:T(128)} %param.27) | copy-start | bytes 580
Sparse Core Ops, SparseCore 0:
  13.9 79.9 all-gather.1
where the time goes:
time: 120 us; the launch traced here: 119 us
  waiting for transfers between devices  57.3 us (48%)
  blocking collectives  22 us (18%)
  local copies, waits for them, and re-layouts  20 us (17%)
  between operations  14.1 us (12%)
  matrix products  4.81 us (4%)
    all_gather x1, waiting for transfers between devices, gather_turned(): whole = lax.all_gather(both, axis, axis=0, tiled=True)  57.3 us
    all_to_all x1, blocking collectives, sent_to_all(): return lax.all_to_all(copies, axis, split_axis=0, concat_axis=0, tiled=True)  22 us
    transpose x1, local copies, waits for them, and re-layouts, gather_turned(): jnp.moveaxis(b.reshape(-1, *t.shape[1:]), 0, dim)  8.13 us
    unnamed x7, local copies, waits for them, and re-layouts  7.37 us
    split x1, local copies, waits for them, and re-layouts, gather_turned(): jnp.split(whole, [sum(widths[:k]) for k in range(1, len(widths))], axis=1)  3.76 us
  transfers between devices with their start and end apart: 1, of which 1 were waited for; matrix products, arithmetic and copies ran while one was open for 1% of the time, Pallas kernels for 0%

commit v1 on v0

--- a/solution.py
+++ b/solution.py
@@ -10,7 +10,9 @@
     turned = [jnp.moveaxis(a, dim, 0) for a, dim in zip(arrays, dims)]
     widths = [t[0].size for t in turned]
     both = jnp.concatenate([t.reshape(-1, w) for t, w in zip(turned, widths)], axis=1)
-    whole = lax.all_gather(both, axis, axis=0, tiled=True)
+    whole = jnp.concatenate(
+        lax.all_to_all(jnp.stack([both] * lax.axis_size(axis)), axis, 0, 0), axis=0
+    )
     tiles = jnp.split(whole, [sum(widths[:k]) for k in range(1, len(widths))], axis=1)
     return tuple(
         (

time: 120 us -> 328 us (2.73)
  waiting for transfers between devices: 57.3 us -> 277 us
  blocking collectives: 22 us -> 0 us
  starting transfers between devices: 0.04 us -> 18.6 us
  between operations: 14.1 us -> 0.69 us
  local copies, waits for them, and re-layouts: 20 us -> 25.9 us
    all_to_all x0 -> x2, waiting for transfers between devices: none -> 277 us  [the longest x1 273 us: gather_turned(): lax.all_to_all(jnp.stack([both] * lax.axis_size(axis)), axis, 0, 0)]
    all_gather x1 -> x0, waiting for transfers between devices: 57.3 us -> none  [gather_turned(): whole = lax.all_gather(both, axis, axis=0, tiled=True)]
    all_to_all x1 -> x0, blocking collectives: 22 us -> none  [sent_to_all(): return lax.all_to_all(copies, axis, split_axis=0, concat_axis=0, tiled=True)]
    all_to_all x0 -> x2, starting transfers between devices: none -> 18.6 us  [the longest x1 13 us: sent_to_all(): return lax.all_to_all(copies, axis, split_axis=0, concat_axis=0, tiled=True)]
    another operation x0 -> x1, local copies, waits for them, and re-layouts: none -> 6.07 us  [gather_turned(): jnp.stack([both] * lax.axis_size(axis))]
    unnamed x7 -> x3, local copies, waits for them, and re-layouts: 7.37 us -> 6.62 us
  transfers between devices with their start and end apart: 1 -> 2, of which waited for: 1 -> 2; matrix products, arithmetic and copies ran while one was open for 1% -> 2% of each run, Pallas kernels for 0% -> 0%
where the time goes in v1:
time: 328 us
  waiting for transfers between devices  277 us (84%)
  local copies, waits for them, and re-layouts  25.9 us (8%)
  starting transfers between devices  18.6 us (6%)
  matrix products  4.81 us (1%)
    all_to_all x1, waiting for transfers between devices, gather_turned(): lax.all_to_all(jnp.stack([both] * lax.axis_size(axis)), axis, 0, 0)  273 us
    all_to_all x1, starting transfers between devices, sent_to_all(): return lax.all_to_all(copies, axis, split_axis=0, concat_axis=0, tiled=True)  13 us
    transpose x1, local copies, waits for them, and re-layouts, gather_turned(): jnp.moveaxis(b.reshape(-1, *t.shape[1:]), 0, dim)  8.13 us
    unnamed x3, local copies, waits for them, and re-layouts  6.62 us
  transfers between devices with their start and end apart: 2, of which 2 were waited for; matrix products, arithmetic and copies ran while one was open for 2% of the time, Pallas kernels for 0%

profile of v1, /device:TPU:1, one launch (start us, length us, event | category | flops | bytes accessed | tf_op | source)
XLA Modules:
  0.0 327.6 jit_solution(16704601228298147631)
XLA Ops:
  0.6 0.0 copy-start
  0.6 0.7 add_convert_fusion
  1.3 0.6 broadcast_in_dim.3
  2.0 13.0 %all-to-all-start.1 = ((bf16[64,1,48]{2,1,0:T(2,128)(2,1)}), bf16[64,1,48]{2,1,0:T(2,128)(2,1)S(1)}, u32[]{:S(2)}, u32[]{:S(2)}) async-start(bf16[64,1,48]{2,1,0:T(2,128)(2,1)} %broadcast_in_dim.3), calls=%async_computation.1 | async-start | bytes 65536 | tf_op jit(solution)/shard_map/all_to_all | solution.py:27
  15.0 0.0 copy-done
  15.0 1.3 fusion.4
  16.2 1.1 fusion.8
  17.4 1.1 fusion.7
  18.5 1.3 fusion.2
  19.8 0.1 pad_maximum_fusion
  19.9 4.2 %all-to-all-done.1 = bf16[64,1,48]{2,1,0:T(2,128)(2,1)S(1)} async-done(((bf16[64,1,48]{2,1,0:T(2,128)(2,1)}), bf16[64,1,48]{2,1,0:T(2,128)(2,1)S(1)}, u32[]{:S(2)}, u32[]{:S(2)}) %all-to-all-start.1) | async-done | bytes 6176 | tf_op jit(solution)/shard_map/all_to_all | solution.py:27
  24.1 6.1 %stack.2 = bf16[16,192,2048]{2,1,0:T(8,128)(2,1)} broadcast(bf16[192,2048]{1,0:T(8,128)(2,1)S(1)} %pad_maximum_fusion), dimensions={1,2} | broadcast | bytes 13369344 | tf_op jit(solution)/shard_map/stack | solution.py:14
  30.1 5.6 %all-to-all-start = ((bf16[16,192,2048]{2,1,0:T(8,128)(2,1)}), bf16[16,192,2048]{2,1,0:T(8,128)(2,1)}, u32[]{:S(2)}, u32[]{:S(2)}) async-start(bf16[16,192,2048]{2,1,0:T(8,128)(2,1)} %stack.2), calls=%async_computation | async-start | bytes 25165824 | tf_op jit(solution)/shard_map/all_to_all | solution.py:14
  35.8 0.1 reduce
  35.8 0.7 reshape.24
  36.5 272.5 %all-to-all-done = bf16[16,192,2048]{2,1,0:T(8,128)(2,1)} async-done(((bf16[16,192,2048]{2,1,0:T(8,128)(2,1)}), bf16[16,192,2048]{2,1,0:T(8,128)(2,1)}, u32[]{:S(2)}, u32[]{:S(2)}) %all-to-all-start) | async-done | bytes 12582944 | tf_op jit(solution)/shard_map/all_to_all | solution.py:14
  309.1 8.1 %slice_bitcast_fusion = (bf16[768,3072]{0,1:T(8,128)(2,1)}, bf16[3072,768]{1,0:T(8,128)(2,1)}) fusion(bf16[3072,2048]{1,0:T(8,128)(2,1)} %bitcast.1), kind=kLoop, calls=%fused_computation | loop fusion | bytes 18874368 | tf_op jit(solution)/shard_map/transpose | solution.py:19
  317.2 3.8 %fusion.9 = (bf16[3072,256]{1,0:T(8,128)(2,1)}, bf16[3072,256]{1,0:T(8,128)(2,1)}) fusion(bf16[3072,2048]{1,0:T(8,128)(2,1)} %bitcast.1), kind=kLoop, calls=%fused_computation.16 | loop fusion | bytes 6291456 | tf_op jit(solution)/shard_map/split | solution.py:16
  321.0 6.6 %copy.24 = bf16[768,3072]{1,0:T(8,128)(2,1)} copy(bf16[768,3072]{0,1:T(8,128)(2,1)} %get-tuple-element.20) | data formatting | bytes 9437184
Async XLA Ops:
  0.6 14.3 %copy-start = (bf16[768,32]{0,1:T(8,128)(2,1)S(1)}, bf16[768,32]{0,1:T(8,128)(2,1)}, u32[]{:S(2)}) copy-start(bf16[768,32]{0,1:T(8,128)(2,1)} %param.24) | copy-start | bytes 147460
  2.0 22.1 %all-to-all-start.1 = ((bf16[64,1,48]{2,1,0:T(2,128)(2,1)}), bf16[64,1,48]{2,1,0:T(2,128)(2,1)S(1)}, u32[]{:S(2)}, u32[]{:S(2)}) async-start(bf16[64,1,48]{2,1,0:T(2,128)(2,1)} %broadcast_in_dim.3), calls=%async_computation.1 | async-start | bytes 65536 | tf_op jit(solution)/shard_map/all_to_all | solution.py:27
  30.1 278.9 %all-to-all-start = ((bf16[16,192,2048]{2,1,0:T(8,128)(2,1)}), bf16[16,192,2048]{2,1,0:T(8,128)(2,1)}, u32[]{:S(2)}, u32[]{:S(2)}) async-start(bf16[16,192,2048]{2,1,0:T(8,128)(2,1)} %stack.2), calls=%async_computation | async-start | bytes 25165824 | tf_op jit(solution)/shard_map/all_to_all | solution.py:14
